TPU v7x, 32 devices: a whole 2x2x4 slice. The times are simulated.
32 devices in a mesh: px: 8 (over z, y), py: 4 (over x, core).
Axes of the slice: x: 2, y: 2, z: 4, core: 2. Of those that a mesh axis runs over, the one named last changes fastest.
Arguments:
- initial_field: float32 [1, 2048, 2048], P(None, ('px', 'py')), may hold values from -6 to 6
- target_field: float32 [1, 2048, 2048], P(None, ('px', 'py')), may hold values from -6 to 6
- forcing: float32 [2, 2048, 2048], P(None, ('px', 'py')), may hold values from -6 to 6
Outputs:
- next_field: float32 [1, 2048, 2048], P(None, ('px', 'py'))
- objective: float32 [], replicated
- field_grad: float32 [1, 2048, 2048], P(None, ('px', 'py'))
- forcing_grad: float32 [2, 2048, 2048], P(None, ('px', 'py'))
All inputs are finite; a program needn't handle non-finite values.
Results may differ from a plain program's by a relative error of at most 0.00014.
Values sent between devices are 32-bit elements; how exact they have to be, the bound alone decides.
A program may use at most 128 MiB of HBM per device.

v0:
```python
import math
import jax
import jax.numpy as jnp
from jax import lax
from jax.sharding import PartitionSpec as P

time_step = 0.25
highest = lax.Precision.HIGHEST


def factor_pair(length):
    first_len = int(math.isqrt(length))
    while length % first_len:
        first_len -= 1
    return (first_len, length // first_len)


def phases(row_count, col_count, period, sign_value, factor):
    product = (
        jnp.arange(row_count, dtype=jnp.int32)[:, None]
        * jnp.arange(col_count, dtype=jnp.int32)[None, :]
        % period
    )
    angles = product.astype(jnp.float32) * (2.0 * math.pi / period)
    return (factor * jnp.cos(angles), sign_value * factor * jnp.sin(angles))


def complex_einsum(formula, left_real, left_imag, table_pair):
    real_term = jnp.einsum(formula, left_real, table_pair[0], precision=highest)
    imag_term = jnp.einsum(formula, left_real, table_pair[1], precision=highest)
    if left_imag is None:
        return (real_term, imag_term)
    real_term = real_term - jnp.einsum(formula, left_imag, table_pair[1], precision=highest)
    imag_term = imag_term + jnp.einsum(formula, left_imag, table_pair[0], precision=highest)
    return (real_term, imag_term)


def transform(real_part, imag_part, sign_value, leading, real_only):
    if leading:
        members, length, span_rows = real_part.shape
        first_len, second_len = factor_pair(length)
        new_shape = (members, first_len, second_len, span_rows)
        formula = "mabr,ak->mrkb"
    else:
        members, span_rows, length = real_part.shape
        first_len, second_len = factor_pair(length)
        new_shape = (members, span_rows, first_len, second_len)
        formula = "mrab,ak->mrkb"
    shaped_real = real_part.reshape(new_shape)
    shaped_imag = None if imag_part is None else imag_part.reshape(new_shape)
    sectioned_out = complex_einsum(
        formula, shaped_real, shaped_imag, phases(first_len, first_len, first_len, sign_value, 1.0)
    )
    twiddle = phases(first_len, second_len, length, sign_value, 1.0 / math.sqrt(length))
    turned_real = sectioned_out[0] * twiddle[0] - sectioned_out[1] * twiddle[1]
    turned_imag = sectioned_out[0] * twiddle[1] + sectioned_out[1] * twiddle[0]
    last_table = phases(second_len, second_len, second_len, sign_value, 1.0)
    final_formula = "mrkb,bq->mrqk"
    if real_only:
        out_real = jnp.einsum(final_formula, turned_real, last_table[0], precision=highest)
        out_real = out_real - jnp.einsum(
            final_formula, turned_imag, last_table[1], precision=highest
        )
        return (out_real.reshape(members, span_rows, length), None)
    out_real, out_imag = complex_einsum(final_formula, turned_real, turned_imag, last_table)
    return (
        out_real.reshape(members, span_rows, length),
        out_imag.reshape(members, span_rows, length),
    )


def regroup(real_part, imag_part):
    moved_real, moved_imag = (
        lax.all_to_all(real_part, ("px", "py"), split_axis=2, concat_axis=1, tiled=True),
        lax.all_to_all(imag_part, ("px", "py"), split_axis=2, concat_axis=1, tiled=True),
    )
    return (moved_real, moved_imag)


def spectral(real_part, imag_part):
    first_pass = transform(real_part, imag_part, -1.0, False, False)
    moved = regroup(first_pass[0], first_pass[1])
    return transform(moved[0], moved[1], -1.0, True, False)


def physical(real_part, imag_part, real_only):
    first_pass = transform(real_part, imag_part, 1.0, False, False)
    moved = regroup(first_pass[0], first_pass[1])
    return transform(moved[0], moved[1], 1.0, True, real_only)


def waves_of(position, count):
    signed = jnp.where(position < count // 2, position, position - count)
    waves = 4.0 * signed.astype(jnp.float32) / count
    derive = jnp.where(position == count // 2, jnp.float32(0.0), waves)
    return (waves, derive)


def per_device(initial_field, target_field, forcing):
    members = initial_field.shape[0]
    full_second = initial_field.shape[2]
    spec_rows = forcing.shape[1]
    full_first = forcing.shape[2]
    device = lax.axis_index(("px", "py"))
    position_first = jnp.arange(full_first, dtype=jnp.int32)
    position_second = device * spec_rows + jnp.arange(spec_rows, dtype=jnp.int32)
    wave_first, deriv_first = waves_of(position_first, full_first)
    wave_second, deriv_second = waves_of(position_second, full_second)
    wave_first = wave_first[None, :]
    deriv_first = deriv_first[None, :]
    wave_second = wave_second[:, None]
    deriv_second = deriv_second[:, None]
    wave_square = wave_first * wave_first + wave_second * wave_second
    denominator = 1.0 + time_step * (wave_square * wave_square - wave_square)
    state_real, state_imag = spectral(initial_field, None)
    slope_real = -deriv_first * state_imag - deriv_second * state_real
    slope_imag = deriv_first * state_real - deriv_second * state_imag
    grad_first, grad_second = physical(slope_real, slope_imag, False)
    nonlinear = -0.5 * (grad_first * grad_first + grad_second * grad_second)
    nonlinear_real, nonlinear_imag = spectral(nonlinear, None)
    next_real = (state_real + time_step * (nonlinear_real + forcing[0])) / denominator
    next_imag = (state_imag + time_step * (nonlinear_imag + forcing[1])) / denominator
    next_field, unused_part = physical(next_real, next_imag, True)
    residual = next_field - target_field
    total = lax.psum(0.5 * jnp.sum(residual * residual), ("px", "py"))
    objective = total / (members * full_first * full_second)
    misfit_real, misfit_imag = spectral(residual, None)
    coef_real = misfit_real / denominator
    coef_imag = misfit_imag / denominator
    forcing_grad = time_step * jnp.stack([jnp.sum(coef_real, axis=0), jnp.sum(coef_imag, axis=0)])
    multiplier, unused_other = physical(time_step * coef_real, time_step * coef_imag, True)
    joint_real, joint_imag = spectral(multiplier * grad_first, multiplier * grad_second)
    total_real = coef_real - deriv_first * joint_imag + deriv_second * joint_real
    total_imag = coef_imag + deriv_first * joint_real + deriv_second * joint_imag
    field_grad, unused_last = physical(total_real, total_imag, True)
    return (next_field, objective, field_grad, forcing_grad)


def solution(mesh):
    return jax.shard_map(
        per_device,
        mesh=mesh,
        in_specs=(
            P(None, ("px", "py"), None),
            P(None, ("px", "py"), None),
            P(None, ("px", "py"), None),
        ),
        out_specs=(
            P(None, ("px", "py"), None),
            P(),
            P(None, ("px", "py"), None),
            P(None, ("px", "py"), None),
        ),
        check_vma=False,
    )
```

profile of v0, /device:TPU:0, one launch (start us, length us, event | category | flops | bytes accessed | tf_op | source)
XLA Modules:
  0.0 883.1 jit_solution(13582286991271843873)
XLA Ops:
  13.7 10.5 %reduce = f32[2048,64]{1,0:T(8,128)S(1)} reduce(f32[2048,1,64]{2,1,0:T(1,128)} %bitcast.931, f32[]{:T(128)} %broadcast.1623), dimensions={1}, to_apply=%bitcast.761.reduce_sub_computation | reduce | bytes 1048580
  25.6 7.3 all-to-all-start
  40.6 9.3 %reduce.2 = f32[2048,64]{1,0:T(8,128)S(1)} reduce(f32[2048,1,64]{2,1,0:T(1,128)S(1)} %bitcast.932, f32[]{:T(128)} %broadcast.1623), dimensions={1}, to_apply=%bitcast.763.reduce_sub_computation | reduce | bytes 1048580
  51.3 6.2 all-to-all-start.1
  65.1 8.1 all-to-all-done.1
  123.8 11.5 %reduce.4 = f32[2048,64]{1,0:T(8,128)} reduce(f32[2048,1,64]{2,1,0:T(1,128)} %bitcast.933, f32[]{:T(128)} %broadcast.1623), dimensions={1}, to_apply=%bitcast.765.reduce_sub_computation | reduce | bytes 1048580
  151.2 10.3 %reduce.6 = f32[2048,64]{1,0:T(8,128)S(1)} reduce(f32[2048,1,64]{2,1,0:T(1,128)} %bitcast.934, f32[]{:T(128)} %broadcast.1623), dimensions={1}, to_apply=%bitcast.767.reduce_sub_computation | reduce | bytes 1048580
  162.9 6.3 all-to-all-start.3
  234.5 11.3 %reduce.8 = f32[2048,64]{1,0:T(8,128)} reduce(f32[2048,1,64]{2,1,0:T(1,128)} %bitcast.935, f32[]{:T(128)} %broadcast.1623), dimensions={1}, to_apply=%bitcast.769.reduce_sub_computation | reduce | bytes 1048580
  262.0 10.3 %reduce.10 = f32[2048,64]{1,0:T(8,128)S(1)} reduce(f32[2048,1,64]{2,1,0:T(1,128)} %bitcast.936, f32[]{:T(128)} %broadcast.1623), dimensions={1}, to_apply=%bitcast.771.reduce_sub_computation | reduce | bytes 1048580
  273.8 6.3 all-to-all-start.5
  349.9 10.3 %reduce.12 = f32[2048,64]{1,0:T(8,128)S(1)} reduce(f32[2048,1,64]{2,1,0:T(1,128)} %bitcast.937, f32[]{:T(128)} %broadcast.1623), dimensions={1}, to_apply=%bitcast.773.reduce_sub_computation | reduce | bytes 1048580
  361.6 6.3 all-to-all-start.6
  375.6 9.3 %reduce.14 = f32[2048,64]{1,0:T(8,128)S(1)} reduce(f32[2048,1,64]{2,1,0:T(1,128)S(1)} %bitcast.938, f32[]{:T(128)} %broadcast.1623), dimensions={1}, to_apply=%bitcast.775.reduce_sub_computation | reduce | bytes 1048580
  386.3 6.2 all-to-all-start.7
  401.2 6.8 all-to-all-done.7
  436.4 10.3 %reduce.16 = f32[2048,64]{1,0:T(8,128)S(1)} reduce(f32[2048,1,64]{2,1,0:T(1,128)} %bitcast.939, f32[]{:T(128)} %broadcast.1623), dimensions={1}, to_apply=%bitcast.777.reduce_sub_computation | reduce | bytes 1048580
  458.7 9.3 %reduce.18 = f32[2048,64]{1,0:T(8,128)S(1)} reduce(f32[2048,1,64]{2,1,0:T(1,128)S(1)} %bitcast.940, f32[]{:T(128)} %broadcast.1623), dimensions={1}, to_apply=%bitcast.779.reduce_sub_computation | reduce | bytes 1048580
  469.4 6.2 all-to-all-start.9
  483.0 8.3 all-to-all-done.9
  542.0 11.3 %reduce.20 = f32[2048,64]{1,0:T(8,128)} reduce(f32[2048,1,64]{2,1,0:T(1,128)} %bitcast.941, f32[]{:T(128)} %broadcast.1623), dimensions={1}, to_apply=%bitcast.781.reduce_sub_computation | reduce | bytes 1048580
  559.5 4.7 fusion.135
  569.3 10.3 %reduce.22 = f32[2048,64]{1,0:T(8,128)S(1)} reduce(f32[2048,1,64]{2,1,0:T(1,128)} %bitcast.942, f32[]{:T(128)} %broadcast.1623), dimensions={1}, to_apply=%bitcast.783.reduce_sub_computation | reduce | bytes 1048580
  581.0 6.3 all-to-all-start.11
  645.4 11.3 %reduce.24 = f32[2048,64]{1,0:T(8,128)} reduce(f32[2048,1,64]{2,1,0:T(1,128)} %bitcast.943, f32[]{:T(128)} %broadcast.1623), dimensions={1}, to_apply=%bitcast.785.reduce_sub_computation | reduce | bytes 1048580
  672.8 10.3 %reduce.26 = f32[2048,64]{1,0:T(8,128)S(1)} reduce(f32[2048,1,64]{2,1,0:T(1,128)} %bitcast.944, f32[]{:T(128)} %broadcast.1623), dimensions={1}, to_apply=%bitcast.787.reduce_sub_computation | reduce | bytes 1048580
  684.5 6.5 all-to-all-start.13
  765.7 11.5 %reduce.28 = f32[2048,64]{1,0:T(8,128)} reduce(f32[2048,1,64]{2,1,0:T(1,128)} %bitcast.945, f32[]{:T(128)} %broadcast.1623), dimensions={1}, to_apply=%bitcast.789.reduce_sub_computation | reduce | bytes 1048580
  783.8 40.5 %psum.7 = f32[]{:T(128)} all-reduce(f32[]{:T(128)S(6)} %mul_shard_map.3), channel_id=1, replica_groups=mesh['px'=8,'py'=4] {'px','py'}, use_global_device_ids=true, to_apply=%region_1.2 | all-reduce | flops 1 | bytes 8 | tf_op jit(solution)/shard_map/psum | solution.py:125
  837.1 10.3 %reduce.30 = f32[2048,64]{1,0:T(8,128)S(1)} reduce(f32[2048,1,64]{2,1,0:T(1,128)} %bitcast.946, f32[]{:T(128)} %broadcast.1623), dimensions={1}, to_apply=%bitcast.791.reduce_sub_computation | reduce | bytes 1048580
  848.9 5.0 all-to-all-start.15
  864.4 5.0 all-to-all-done.15
  (350 shorter events, 574.7 us)
Async XLA Ops:
  25.6 25.7 %all-to-all-start = ((f32[32,1,4096]{2,1,0:T(1,128)}), f32[32,1,4096]{2,1,0:T(1,128)S(1)}, u32[]{:S(2)}, u32[]{:S(2)}) async-start(f32[32,1,4096]{2,1,0:T(1,128)} %reshape.1269), calls=%async_computation | async-start | bytes 1048576 | tf_op jit(solution)/shard_map/all_to_all | solution.py:74
  51.3 21.9 %all-to-all-start.1 = ((f32[32,1,4096]{2,1,0:T(1,128)}), f32[32,1,4096]{2,1,0:T(1,128)S(1)}, u32[]{:S(2)}, u32[]{:S(2)}) async-start(f32[32,1,4096]{2,1,0:T(1,128)} %reshape.1271), calls=%async_computation.1 | async-start | bytes 1048576 | tf_op jit(solution)/shard_map/all_to_all | solution.py:75
  115.2 7.1 copy-start.10
  138.0 24.9 %all-to-all-start.2 = ((f32[32,1,4096]{2,1,0:T(1,128)}), f32[32,1,4096]{2,1,0:T(1,128)}, u32[]{:S(2)}, u32[]{:S(2)}) async-start(f32[32,1,4096]{2,1,0:T(1,128)} %reshape.1273), calls=%async_computation.2 | async-start | bytes 1048576 | tf_op jit(solution)/shard_map/all_to_all | solution.py:74
  162.9 21.9 %all-to-all-start.3 = ((f32[32,1,4096]{2,1,0:T(1,128)}), f32[32,1,4096]{2,1,0:T(1,128)}, u32[]{:S(2)}, u32[]{:S(2)}) async-start(f32[32,1,4096]{2,1,0:T(1,128)} %reshape.1275), calls=%async_computation.3 | async-start | bytes 1048576 | tf_op jit(solution)/shard_map/all_to_all | solution.py:75
  192.2 2.4 copy-start.31
  209.5 4.5 copy-start.24
  214.0 3.5 copy-start.4
  225.7 7.2 copy-start.13
  248.5 25.3 %all-to-all-start.4 = ((f32[32,1,4096]{2,1,0:T(1,128)}), f32[32,1,4096]{2,1,0:T(1,128)}, u32[]{:S(2)}, u32[]{:S(2)}) async-start(f32[32,1,4096]{2,1,0:T(1,128)} %reshape.1277), calls=%async_computation.4 | async-start | bytes 1048576 | tf_op jit(solution)/shard_map/all_to_all | solution.py:74
  273.8 21.8 %all-to-all-start.5 = ((f32[32,1,4096]{2,1,0:T(1,128)}), f32[32,1,4096]{2,1,0:T(1,128)}, u32[]{:S(2)}, u32[]{:S(2)}) async-start(f32[32,1,4096]{2,1,0:T(1,128)} %reshape.1279), calls=%async_computation.5 | async-start | bytes 1048576 | tf_op jit(solution)/shard_map/all_to_all | solution.py:75
  303.0 2.4 copy-start.32
  320.5 5.1 copy-start.20
  325.6 3.8 copy-start.15
  325.7 3.8 copy-start.16
  361.6 24.7 %all-to-all-start.6 = ((f32[32,1,4096]{2,1,0:T(1,128)}), f32[32,1,4096]{2,1,0:T(1,128)}, u32[]{:S(2)}, u32[]{:S(2)}) async-start(f32[32,1,4096]{2,1,0:T(1,128)} %reshape.1281), calls=%async_computation.6 | async-start | bytes 1048576 | tf_op jit(solution)/shard_map/all_to_all | solution.py:74
  384.8 7.7 copy-start.37
  386.3 21.7 %all-to-all-start.7 = ((f32[32,1,4096]{2,1,0:T(1,128)}), f32[32,1,4096]{2,1,0:T(1,128)}, u32[]{:S(2)}, u32[]{:S(2)}) async-start(f32[32,1,4096]{2,1,0:T(1,128)} %reshape.1283), calls=%async_computation.7 | async-start | bytes 1048576 | tf_op jit(solution)/shard_map/all_to_all | solution.py:75
  448.1 21.3 %all-to-all-start.8 = ((f32[32,1,4096]{2,1,0:T(1,128)}), f32[32,1,4096]{2,1,0:T(1,128)S(1)}, u32[]{:S(2)}, u32[]{:S(2)}) async-start(f32[32,1,4096]{2,1,0:T(1,128)} %reshape.1285), calls=%async_computation.8 | async-start | bytes 1048576 | tf_op jit(solution)/shard_map/all_to_all | solution.py:74
  469.4 21.9 %all-to-all-start.9 = ((f32[32,1,4096]{2,1,0:T(1,128)}), f32[32,1,4096]{2,1,0:T(1,128)S(1)}, u32[]{:S(2)}, u32[]{:S(2)}) async-start(f32[32,1,4096]{2,1,0:T(1,128)} %reshape.1287), calls=%async_computation.9 | async-start | bytes 1048576 | tf_op jit(solution)/shard_map/all_to_all | solution.py:75
  533.3 7.0 copy-start.11
  555.9 25.1 %all-to-all-start.10 = ((f32[32,1,4096]{2,1,0:T(1,128)}), f32[32,1,4096]{2,1,0:T(1,128)}, u32[]{:S(2)}, u32[]{:S(2)}) async-start(f32[32,1,4096]{2,1,0:T(1,128)} %reshape.1289), calls=%async_computation.10 | async-start | bytes 1048576 | tf_op jit(solution)/shard_map/all_to_all | solution.py:74
  581.0 21.7 %all-to-all-start.11 = ((f32[32,1,4096]{2,1,0:T(1,128)}), f32[32,1,4096]{2,1,0:T(1,128)}, u32[]{:S(2)}, u32[]{:S(2)}) async-start(f32[32,1,4096]{2,1,0:T(1,128)} %reshape.1291), calls=%async_computation.11 | async-start | bytes 1048576 | tf_op jit(solution)/shard_map/all_to_all | solution.py:75
  610.0 2.4 copy-start.35
  622.7 4.2 copy-start.36
  636.6 7.2 copy-start.9
  659.4 25.1 %all-to-all-start.12 = ((f32[32,1,4096]{2,1,0:T(1,128)}), f32[32,1,4096]{2,1,0:T(1,128)}, u32[]{:S(2)}, u32[]{:S(2)}) async-start(f32[32,1,4096]{2,1,0:T(1,128)} %reshape.1293), calls=%async_computation.12 | async-start | bytes 1048576 | tf_op jit(solution)/shard_map/all_to_all | solution.py:74
  684.5 22.1 %all-to-all-start.13 = ((f32[32,1,4096]{2,1,0:T(1,128)}), f32[32,1,4096]{2,1,0:T(1,128)}, u32[]{:S(2)}, u32[]{:S(2)}) async-start(f32[32,1,4096]{2,1,0:T(1,128)} %reshape.1295), calls=%async_computation.13 | async-start | bytes 1048576 | tf_op jit(solution)/shard_map/all_to_all | solution.py:75
  731.2 5.1 copy-start.23
  757.0 7.0 copy-start.8
  779.8 69.1 %all-to-all-start.14 = ((f32[32,1,4096]{2,1,0:T(1,128)}), f32[32,1,4096]{2,1,0:T(1,128)}, u32[]{:S(2)}, u32[]{:S(2)}) async-start(f32[32,1,4096]{2,1,0:T(1,128)} %reshape.1297), calls=%async_computation.14 | async-start | bytes 1048576 | tf_op jit(solution)/shard_map/all_to_all | solution.py:74
  848.9 20.5 %all-to-all-start.15 = ((f32[32,1,4096]{2,1,0:T(1,128)}), f32[32,1,4096]{2,1,0:T(1,128)S(1)}, u32[]{:S(2)}, u32[]{:S(2)}) async-start(f32[32,1,4096]{2,1,0:T(1,128)} %reshape.1299), calls=%async_computation.15 | async-start | bytes 1048576 | tf_op jit(solution)/shard_map/all_to_all | solution.py:75
  (22 other events, 35.2 us)
where the time goes:
time: 894 us; the launch traced here: 883 us
  matrix products  321 us (36%)
  other arithmetic  217 us (24%)
  local copies, waits for them, and re-layouts  176 us (20%)
  starting transfers between devices  83.1 us (9%)
  blocking collectives  40.5 us (5%)
  waiting for transfers between devices  40.4 us (5%)
    unnamed x16, other arithmetic  167 us
    dot_general x29, matrix products, complex_einsum(): imag_term = jnp.einsum(formula, left_real, table_pair[1], precision=highest)  81.2 us
    dot_general x29, matrix products, complex_einsum(): real_term = jnp.einsum(formula, left_real, table_pair[0], precision=highest)  80 us
    unnamed x115, local copies, waits for them, and re-layouts  74.6 us
    dot_general x26, matrix products, complex_einsum(): jnp.einsum(formula, left_imag, table_pair[1], precision=highest)  74.2 us
    dot_general x26, matrix products, complex_einsum(): jnp.einsum(formula, left_imag, table_pair[0], precision=highest)  73.5 us
    all_to_all x8, starting transfers between devices, regroup(): lax.all_to_all(imag_part, ('px', 'py'), split_axis=2, concat_axis=1, tile...  49.1 us
    psum x1, blocking collectives, per_device(): total = lax.psum(0.5 * jnp.sum(residual * residual), ('px', 'py'))  40.5 us
  transfers between devices with their start and end apart: 16, of which 8 were waited for; matrix products, arithmetic and copies ran while one was open for 28% of the time, Pallas kernels for 0%

commit v1 on v0

--- a/solution.py
+++ b/solution.py
@@ -72,7 +72,15 @@
 def regroup(real_part, imag_part):
     moved_real, moved_imag = (
         lax.all_to_all(real_part, ("px", "py"), split_axis=2, concat_axis=1, tiled=True),
-        lax.all_to_all(imag_part, ("px", "py"), split_axis=2, concat_axis=1, tiled=True),
+        jnp.concatenate(
+            lax.all_to_all(
+                jnp.stack(jnp.split(imag_part, lax.axis_size(("px", "py")), axis=2)),
+                ("px", "py"),
+                0,
+                0,
+            ),
+            axis=1,
+        ),
     )
     return (moved_real, moved_imag)
 

time: 894 us -> 941 us (1.053)
  local copies, waits for them, and re-layouts: 176 us -> 262 us
  other arithmetic: 217 us -> 150 us
  waiting for transfers between devices: 40.4 us -> 62.4 us
  matrix products: 321 us -> 332 us
    unnamed x115 -> x351, local copies, waits for them, and re-layouts: 74.6 us -> 166 us
    unnamed x16 -> x8, other arithmetic: 167 us -> 89.4 us
    all_to_all x8, waiting for transfers between devices: 0.02 us -> 24.3 us  [regroup(): lax.all_to_all(real_part, ('px', 'py'), split_axis=2, concat_axis=1, tile...]
    dot_general x26, matrix products: 73.5 us -> 88.7 us  [complex_einsum(): jnp.einsum(formula, left_imag, table_pair[0], precision=highest)]
    all_to_all x8 -> x0, local copies, waits for them, and re-layouts: 13.5 us -> none  [regroup(): lax.all_to_all(imag_part, ('px', 'py'), split_axis=2, concat_axis=1, tile...]
    another operation x13 -> x29, local copies, waits for them, and re-layouts: 19.6 us -> 32.5 us
    all_to_all x8, other arithmetic: 19.8 us -> 30.2 us  [regroup(): lax.all_to_all(jnp.stack(jnp.split(imag_part, lax.axis_size(('px', 'py'))...]
  transfers between devices with their start and end apart: 16 -> 16, of which waited for: 8 -> 10; matrix products, arithmetic and copies ran while one was open for 28% -> 26% of each run, Pallas kernels for 0% -> 0%
where the time goes in v1:
time: 941 us; the launch traced here: 929 us
  matrix products  332 us (35%)
  local copies, waits for them, and re-layouts  262 us (28%)
  other arithmetic  150 us (16%)
  starting transfers between devices  76 us (8%)
  waiting for transfers between devices  62.4 us (7%)
  blocking collectives  40.7 us (4%)
    unnamed x351, local copies, waits for them, and re-layouts  166 us
    unnamed x8, other arithmetic  89.4 us
    dot_general x26, matrix products, complex_einsum(): jnp.einsum(formula, left_imag, table_pair[0], precision=highest)  88.7 us
    dot_general x29, matrix products, complex_einsum(): imag_term = jnp.einsum(formula, left_real, table_pair[1], precision=highest)  79.9 us
    dot_general x29, matrix products, complex_einsum(): real_term = jnp.einsum(formula, left_real, table_pair[0], precision=highest)  76.8 us
    dot_general x26, matrix products, complex_einsum(): jnp.einsum(formula, left_imag, table_pair[1], precision=highest)  75.1 us
    all_to_all x8, starting transfers between devices, regroup(): lax.all_to_all(jnp.stack(jnp.split(imag_part, lax.axis_size(('px', 'py'))...  41.8 us
    psum x1, blocking collectives, per_device(): total = lax.psum(0.5 * jnp.sum(residual * residual), ('px', 'py'))  40.7 us
  transfers between devices with their start and end apart: 16, of which 10 were waited for; matrix products, arithmetic and copies ran while one was open for 26% of the time, Pallas kernels for 0%

profile of v1, /device:TPU:0, one launch (start us, length us, event | category | flops | bytes accessed | tf_op | source)
XLA Modules:
  0.0 929.2 jit_solution(7373497950666213398)
XLA Ops:
  13.7 10.7 %reduce = f32[2048,64]{1,0:T(8,128)S(1)} reduce(f32[2048,1,64]{2,1,0:T(1,128)} %bitcast.2155, f32[]{:T(128)} %broadcast.1623), dimensions={1}, to_apply=%bitcast.1745.reduce_sub_computation | reduce | bytes 1048580
  25.9 7.3 all-to-all-start
  43.1 5.8 all-to-all-done
  59.4 8.9 all-to-all-done.1
  125.8 11.4 %reduce.3 = f32[2048,64]{1,0:T(8,128)} reduce(f32[2048,1,64]{2,1,0:T(1,128)} %bitcast.2156, f32[]{:T(128)} %broadcast.1623), dimensions={1}, to_apply=%bitcast.1747.reduce_sub_computation | reduce | bytes 1048580
  143.3 4.7 fusion.42
  171.4 6.1 all-to-all-start.3
  216.8 4.5 convolution_add_fusion.19
  246.5 11.6 %reduce.6 = f32[2048,64]{1,0:T(8,128)} reduce(f32[2048,1,64]{2,1,0:T(1,128)} %bitcast.2157, f32[]{:T(128)} %broadcast.1623), dimensions={1}, to_apply=%bitcast.1749.reduce_sub_computation | reduce | bytes 1048580
  264.1 4.7 fusion.38
  292.3 6.1 all-to-all-start.5
  338.0 4.5 fusion.34
  370.8 10.6 %reduce.9 = f32[2048,64]{1,0:T(8,128)S(1)} reduce(f32[2048,1,64]{2,1,0:T(1,128)} %bitcast.2158, f32[]{:T(128)} %broadcast.1623), dimensions={1}, to_apply=%bitcast.1751.reduce_sub_computation | reduce | bytes 1048580
  382.9 5.9 all-to-all-start.6
  395.1 9.3 all-to-all-done.6
  417.7 6.4 all-to-all-done.7
  454.6 10.4 %reduce.12 = f32[2048,64]{1,0:T(8,128)S(1)} reduce(f32[2048,1,64]{2,1,0:T(1,128)} %bitcast.2159, f32[]{:T(128)} %broadcast.1623), dimensions={1}, to_apply=%bitcast.1753.reduce_sub_computation | reduce | bytes 1048580
  475.8 9.3 all-to-all-done.8
  495.2 9.2 all-to-all-done.9
  561.7 11.8 %reduce.15 = f32[2048,64]{1,0:T(8,128)} reduce(f32[2048,1,64]{2,1,0:T(1,128)} %bitcast.2160, f32[]{:T(128)} %broadcast.1623), dimensions={1}, to_apply=%bitcast.1755.reduce_sub_computation | reduce | bytes 1048580
  579.5 4.7 fusion.17
  607.2 6.1 all-to-all-start.11
  664.9 4.6 fusion.133
  674.7 11.4 %reduce.18 = f32[2048,64]{1,0:T(8,128)} reduce(f32[2048,1,64]{2,1,0:T(1,128)} %bitcast.2161, f32[]{:T(128)} %broadcast.1623), dimensions={1}, to_apply=%bitcast.1757.reduce_sub_computation | reduce | bytes 1048580
  692.1 4.7 fusion.11
  722.1 5.9 all-to-all-start.13
  728.6 40.7 %psum.7 = f32[]{:T(128)} all-reduce(f32[]{:T(128)S(6)} %mul_shard_map.3), channel_id=1, replica_groups=mesh['px'=8,'py'=4] {'px','py'}, use_global_device_ids=true, to_apply=%region_1.2 | all-reduce | flops 1 | bytes 8 | tf_op jit(solution)/shard_map/psum | solution.py:133
  845.4 11.4 %reduce.21 = f32[2048,64]{1,0:T(8,128)} reduce(f32[2048,1,64]{2,1,0:T(1,128)} %bitcast.2162, f32[]{:T(128)} %broadcast.1623), dimensions={1}, to_apply=%bitcast.1759.reduce_sub_computation | reduce | bytes 1048580
  859.5 4.8 all-to-all-start.14
  864.3 4.7 fusion.3
  892.4 6.3 all-to-all-start.15
  908.2 5.6 all-to-all-done.15
  (586 shorter events, 653.5 us)
Async XLA Ops:
  25.9 23.0 %all-to-all-start = ((f32[32,1,4096]{2,1,0:T(1,128)}), f32[32,1,4096]{2,1,0:T(1,128)S(1)}, u32[]{:S(2)}, u32[]{:S(2)}) async-start(f32[32,1,4096]{2,1,0:T(1,128)} %reshape.1277), calls=%async_computation | async-start | bytes 1048576 | tf_op jit(solution)/shard_map/all_to_all | solution.py:74
  48.9 19.5 %all-to-all-start.1 = ((f32[32,1,4096]{2,1,0:T(1,128)}), f32[32,1,4096]{2,1,0:T(1,128)}, u32[]{:S(2)}, u32[]{:S(2)}) async-start(f32[32,1,4096]{2,1,0:T(1,128)} %reshape.1279), calls=%async_computation.1 | async-start | bytes 1048576 | tf_op jit(solution)/shard_map/all_to_all | solution.py:76
  107.3 2.4 copy-start.15
  139.9 31.5 %all-to-all-start.2 = ((f32[32,1,4096]{2,1,0:T(1,128)}), f32[32,1,4096]{2,1,0:T(1,128)}, u32[]{:S(2)}, u32[]{:S(2)}) async-start(f32[32,1,4096]{2,1,0:T(1,128)} %reshape.1281), calls=%async_computation.2 | async-start | bytes 1048576 | tf_op jit(solution)/shard_map/all_to_all | solution.py:74
  171.4 21.7 %all-to-all-start.3 = ((f32[32,1,4096]{2,1,0:T(1,128)}), f32[32,1,4096]{2,1,0:T(1,128)}, u32[]{:S(2)}, u32[]{:S(2)}) async-start(f32[32,1,4096]{2,1,0:T(1,128)} %reshape.1283), calls=%async_computation.3 | async-start | bytes 1048576 | tf_op jit(solution)/shard_map/all_to_all | solution.py:76
  198.3 3.0 copy-start.25
  216.8 4.5 copy-start.20
  221.3 3.5 copy-start.4
  260.8 31.5 %all-to-all-start.4 = ((f32[32,1,4096]{2,1,0:T(1,128)}), f32[32,1,4096]{2,1,0:T(1,128)}, u32[]{:S(2)}, u32[]{:S(2)}) async-start(f32[32,1,4096]{2,1,0:T(1,128)} %reshape.1285), calls=%async_computation.4 | async-start | bytes 1048576 | tf_op jit(solution)/shard_map/all_to_all | solution.py:74
  292.3 21.7 %all-to-all-start.5 = ((f32[32,1,4096]{2,1,0:T(1,128)}), f32[32,1,4096]{2,1,0:T(1,128)}, u32[]{:S(2)}, u32[]{:S(2)}) async-start(f32[32,1,4096]{2,1,0:T(1,128)} %reshape.1287), calls=%async_computation.5 | async-start | bytes 1048576 | tf_op jit(solution)/shard_map/all_to_all | solution.py:76
  319.2 3.0 copy-start.26
  338.0 5.1 copy-start.16
  343.1 3.8 copy-start.11
  343.1 3.8 copy-start.12
  382.9 21.5 %all-to-all-start.6 = ((f32[32,1,4096]{2,1,0:T(1,128)}), f32[32,1,4096]{2,1,0:T(1,128)S(1)}, u32[]{:S(2)}, u32[]{:S(2)}) async-start(f32[32,1,4096]{2,1,0:T(1,128)} %reshape.1289), calls=%async_computation.6 | async-start | bytes 1048576 | tf_op jit(solution)/shard_map/all_to_all | solution.py:74
  393.7 15.3 %copy-start.31 = (f32[1,64,2048]{2,1,0:T(8,128)S(1)}, f32[1,64,2048]{2,1,0:T(8,128)}, u32[]{:S(2)}) copy-start(f32[1,64,2048]{2,1,0:T(8,128)} %param.4) | copy-start | bytes 1572868
  405.2 18.9 %all-to-all-start.7 = ((f32[32,1,4096]{2,1,0:T(1,128)}), f32[32,1,4096]{2,1,0:T(1,128)}, u32[]{:S(2)}, u32[]{:S(2)}) async-start(f32[32,1,4096]{2,1,0:T(1,128)} %reshape.1291), calls=%async_computation.7 | async-start | bytes 1048576 | tf_op jit(solution)/shard_map/all_to_all | solution.py:76
  466.5 18.5 %all-to-all-start.8 = ((f32[32,1,4096]{2,1,0:T(1,128)}), f32[32,1,4096]{2,1,0:T(1,128)S(1)}, u32[]{:S(2)}, u32[]{:S(2)}) async-start(f32[32,1,4096]{2,1,0:T(1,128)} %reshape.1293), calls=%async_computation.8 | async-start | bytes 1048576 | tf_op jit(solution)/shard_map/all_to_all | solution.py:74
  485.0 19.3 %all-to-all-start.9 = ((f32[32,1,4096]{2,1,0:T(1,128)}), f32[32,1,4096]{2,1,0:T(1,128)}, u32[]{:S(2)}, u32[]{:S(2)}) async-start(f32[32,1,4096]{2,1,0:T(1,128)} %reshape.1295), calls=%async_computation.9 | async-start | bytes 1048576 | tf_op jit(solution)/shard_map/all_to_all | solution.py:76
  543.5 2.4 copy-start.18
  576.1 31.1 %all-to-all-start.10 = ((f32[32,1,4096]{2,1,0:T(1,128)}), f32[32,1,4096]{2,1,0:T(1,128)}, u32[]{:S(2)}, u32[]{:S(2)}) async-start(f32[32,1,4096]{2,1,0:T(1,128)} %reshape.1297), calls=%async_computation.10 | async-start | bytes 1048576 | tf_op jit(solution)/shard_map/all_to_all | solution.py:74
  607.2 21.5 %all-to-all-start.11 = ((f32[32,1,4096]{2,1,0:T(1,128)}), f32[32,1,4096]{2,1,0:T(1,128)}, u32[]{:S(2)}, u32[]{:S(2)}) async-start(f32[32,1,4096]{2,1,0:T(1,128)} %reshape.1299), calls=%async_computation.11 | async-start | bytes 1048576 | tf_op jit(solution)/shard_map/all_to_all | solution.py:76
  633.9 3.0 copy-start.28
  647.5 4.2 copy-start.29
  688.7 33.4 %all-to-all-start.12 = ((f32[32,1,4096]{2,1,0:T(1,128)}), f32[32,1,4096]{2,1,0:T(1,128)}, u32[]{:S(2)}, u32[]{:S(2)}) async-start(f32[32,1,4096]{2,1,0:T(1,128)} %reshape.1301), calls=%async_computation.12 | async-start | bytes 1048576 | tf_op jit(solution)/shard_map/all_to_all | solution.py:74
  716.8 52.6 %copy-start.9 = (f32[1,64,64,32]{1,3,2,0:T(8,128)S(1)}, f32[1,64,64,32]{1,3,2,0:T(8,128)}, u32[]{:S(2)}) copy-start(f32[1,64,64,32]{1,3,2,0:T(8,128)} %copy-done.8) | copy-start | bytes 1572868
  722.1 60.6 %all-to-all-start.13 = ((f32[32,1,4096]{2,1,0:T(1,128)}), f32[32,1,4096]{2,1,0:T(1,128)}, u32[]{:S(2)}, u32[]{:S(2)}) async-start(f32[32,1,4096]{2,1,0:T(1,128)} %reshape.1303), calls=%async_computation.13 | async-start | bytes 1048576 | tf_op jit(solution)/shard_map/all_to_all | solution.py:76
  787.9 3.0 copy-start.24
  806.7 5.1 copy-start.19
  827.1 2.4 copy-start.14
  859.5 32.9 %all-to-all-start.14 = ((f32[32,1,4096]{2,1,0:T(1,128)}), f32[32,1,4096]{2,1,0:T(1,128)}, u32[]{:S(2)}, u32[]{:S(2)}) async-start(f32[32,1,4096]{2,1,0:T(1,128)} %reshape.1305), calls=%async_computation.14 | async-start | bytes 1048576 | tf_op jit(solution)/shard_map/all_to_all | solution.py:74
  892.4 21.5 %all-to-all-start.15 = ((f32[32,1,4096]{2,1,0:T(1,128)}), f32[32,1,4096]{2,1,0:T(1,128)}, u32[]{:S(2)}, u32[]{:S(2)}) async-start(f32[32,1,4096]{2,1,0:T(1,128)} %reshape.1307), calls=%async_computation.15 | async-start | bytes 1048576 | tf_op jit(solution)/shard_map/all_to_all | solution.py:76
  (16 other events, 23.0 us)
